TPU v7x, 32 devices: a whole 2x2x4 slice. The times are simulated.
32 devices in a mesh: seq: 8 (over z, x), ch: 4 (over y, core).
Axes of the slice: x: 2, y: 2, z: 4, core: 2. Of those that a mesh axis runs over, the one named last changes fastest.
Arguments:
- values: float32 [2048, 1024], P('seq', 'ch'), may hold values from -6 to 6
- gates: float32 [2048, 1024], P('seq', 'ch'), may hold values from -6 to 6
- filter_taps: float32 [4096, 1024], P('seq', 'ch'), may hold values from -0.09375 to 0.09375
- skip: float32 [1024], P('ch'), may hold values from 0.5 to 2
- out_weight: bfloat16 [1024, 2048], P(None, 'ch'), may hold values from -0.1875 to 0.1875
Outputs:
- mixed: float32 [2048, 2048], P('seq', 'ch')
All inputs are finite; a program needn't handle non-finite values.
Results may differ from a plain program's by a relative error of at most 0.0058.
Values may be sent and summed in bfloat16 or wider, within the bound.
A program may use at most 64 MiB of HBM per device.

v0:
```python
import math

import jax
import jax.numpy as jnp
from jax import lax
from jax.sharding import PartitionSpec as P

HIGHEST = lax.Precision.HIGHEST


def split_length(length):
    leading = 1
    for factor in range(1, math.isqrt(length) + 1):
        if length % factor == 0:
            leading = factor
    return (leading, length // leading)


def phase_table(count_rows, count_cols, modulus):
    row_ids = jnp.arange(count_rows, dtype=jnp.int32)
    col_ids = jnp.arange(count_cols, dtype=jnp.int32)
    wrapped = row_ids[:, None] * col_ids[None, :] % modulus
    phases = 2.0 * math.pi / modulus * wrapped.astype(jnp.float32)
    return (jnp.cos(phases), jnp.sin(phases))


def complex_form(cosine, sine):
    upper = jnp.stack([cosine, -sine], axis=1)
    lower = jnp.stack([sine, cosine], axis=1)
    return jnp.stack([upper, lower], axis=0)


def transform_tables(length):
    rows_lead, rows_tail = split_length(length)
    cos_lead, sin_lead = phase_table(rows_lead, rows_lead, rows_lead)
    cos_tail, sin_tail = phase_table(rows_tail, rows_tail, rows_tail)
    cos_twist, sin_twist = phase_table(rows_lead, rows_tail, length)
    lead_table = jnp.stack([cos_lead, -sin_lead])
    tail_forward = complex_form(cos_tail, -sin_tail)
    tail_inverse = complex_form(cos_tail, sin_tail)
    return (
        lead_table,
        tail_forward,
        tail_inverse,
        cos_twist,
        sin_twist,
        rows_lead,
        rows_tail,
        length,
    )


def twist_rows(section, cosine, sine):
    real_part = section[0] * cosine[None] - section[1] * sine[None]
    imag_part = section[0] * sine[None] + section[1] * cosine[None]
    return jnp.stack([real_part, imag_part])


def forward_rows(rows, tables):
    lead_table, tail_forward, tail_inverse, cos_twist, sin_twist, rows_lead, rows_tail, length = (
        tables
    )
    signal = jnp.concatenate([rows, jnp.zeros_like(rows)], axis=1).reshape(
        rows.shape[0], rows_lead, rows_tail
    )
    section = jnp.einsum("pft,cts->pcfs", lead_table, signal, precision=HIGHEST)
    twisted = twist_rows(section, cos_twist, -sin_twist)
    return jnp.einsum("pgrs,rcfs->pcfg", tail_forward, twisted, precision=HIGHEST)


def inverse_rows(spectrum, tables):
    lead_table, tail_forward, tail_inverse, cos_twist, sin_twist, rows_lead, rows_tail, length = (
        tables
    )
    section = jnp.einsum("pgrs,rcfs->pcfg", tail_inverse, spectrum, precision=HIGHEST)
    twisted = twist_rows(section, cos_twist, sin_twist)
    signal = jnp.einsum("rft,rcfs->cts", lead_table, twisted, precision=HIGHEST) / length
    return signal.reshape(signal.shape[0], length)


def product(left, right):
    real_part = left[0] * right[0] - left[1] * right[1]
    imag_part = left[0] * right[1] + left[1] * right[0]
    return jnp.stack([real_part, imag_part])


def body(values, gates, filter_taps, skip, out_weight):
    block_rows, width = values.shape
    whole_filter = lax.all_gather(filter_taps, "seq", axis=0, tiled=True)
    devices = lax.axis_size("seq")
    narrow = width // devices
    whole_rows = lax.all_to_all(values.T, "seq", split_axis=0, concat_axis=1, tiled=True)
    total_rows = whole_rows.shape[1]
    own_taps = lax.dynamic_slice_in_dim(whole_filter, lax.axis_index("seq") * narrow, narrow, 1).T
    used_taps = min(own_taps.shape[1], total_rows)
    own_taps = own_taps[:, :used_taps]
    taps_rows = jnp.concatenate(
        [own_taps, jnp.zeros((narrow, total_rows - used_taps), jnp.float32)], axis=1
    )
    row_tables = transform_tables(2 * total_rows)
    spectrum = product(forward_rows(whole_rows, row_tables), forward_rows(taps_rows, row_tables))
    convolved_rows = inverse_rows(spectrum, row_tables)[:, :total_rows]
    convolved = lax.all_to_all(convolved_rows, "seq", split_axis=1, concat_axis=0, tiled=True).T
    hidden = (gates * (convolved + skip[None, :] * values)).astype(jnp.bfloat16)
    return jnp.dot(
        lax.all_gather(hidden, "ch", axis=1, tiled=True),
        out_weight,
        preferred_element_type=jnp.float32,
    )


def solution(mesh):
    placed = (P("seq", "ch"), P("seq", "ch"), P("seq", "ch"), P("ch"), P(None, "ch"))
    return jax.shard_map(
        body, mesh=mesh, in_specs=placed, out_specs=P("seq", "ch"), check_vma=False
    )
```

profile of v0, /device:TPU:1, one launch (start us, length us, event | category | flops | bytes accessed | tf_op | source)
XLA Modules:
  0.0 139.5 jit_solution(14800312049470740787)
XLA Ops:
  6.5 0.0 copy-start
  6.5 0.0 all-gather.2.cloned.1.call-start
  6.5 0.7 all-gather.2.cloned.1.call-update
  7.3 1.8 %copy.21 = f32[256,256]{0,1:T(8,128)} copy(f32[256,256]{1,0:T(8,128)} %param.5) | data formatting | bytes 524288 | tf_op args[0]
  9.0 6.3 %all-to-all-start = ((f32[8,32,256]{2,1,0:T(8,128)}), f32[8,32,256]{2,1,0:T(8,128)S(1)}, u32[]{:S(2)}, u32[]{:S(2)}) async-start(f32[8,32,256]{2,1,0:T(8,128)} %bitcast.1), calls=%async_computation | async-start | bytes 524288 | tf_op jit(solution)/shard_map/all_to_all | solution.py:92
  15.4 0.1 fusion.58
  15.5 0.1 sine_negate_fusion
  15.7 0.1 fusion.54
  15.8 0.8 fusion.55
  16.6 0.1 fusion.52
  16.8 6.0 %all-to-all-done = f32[8,32,256]{2,1,0:T(8,128)S(1)} async-done(((f32[8,32,256]{2,1,0:T(8,128)}), f32[8,32,256]{2,1,0:T(8,128)S(1)}, u32[]{:S(2)}, u32[]{:S(2)}) %all-to-all-start) | async-done | bytes 262176 | tf_op jit(solution)/shard_map/all_to_all | solution.py:92
  22.9 0.0 copy-start.4
  22.9 0.4 reshape.211
  23.3 3.2 %convolution_bitcast_fusion.1 = f32[2,32,64,64]{2,3,0,1:T(8,128)} fusion(f32[32,64,64]{2,1,0:T(8,128)S(1)} %reshape.211, f32[1,64,64]{2,1,0:T(8,128)S(1)} %get-tuple-element.21, f32[1,64,64]{2,1,0:T(8,128)S(1)} %get-tuple-element.22), kind=kOutput, calls=%fused_computation.21 | convolution fusion | flops 201334784 | bytes 1605632 | tf_op jit(solution)/shard_map/pft,cts->pcfs/dot_general | solution.py:66
  26.5 57.6 %all-gather.2.cloned.1.call-done = f32[4096,256]{1,0:T(8,128)} async-done(((f32[512,256]{1,0:T(8,128)}), f32[4096,256]{1,0:T(8,128)}) %all-gather.2.cloned.1.call-update) | async-done | bytes 4194320 | tf_op jit(solution)/shard_map/all_gather | solution.py:89
  84.2 0.0 copy-done.4
  84.2 4.0 %dynamic-slice_select_fusion = f32[4096,32]{1,0:T(8,128)S(1)} fusion(f32[4096,256]{1,0:T(8,128)} %all-gather.2.cloned.1.call-done, s32[]{:T(128)S(6)} %select_n.96, pred[4096]{0:T(1024)(128)(4,1)S(1)} %copy-done.4), kind=kLoop, calls=%fused_computation.16 | loop fusion | flops 131072 | bytes 1052676 | tf_op jit(solution)/shard_map/concatenate | solution.py:63
  88.1 2.4 %copy.35 = f32[32,64,64,1]{1,2,3,0:T(8,128)} copy(f32[32,64,64,1]{0,2,1,3:T(8,128)S(1)} %bitcast.101) | data formatting | bytes 1048576 | tf_op jit(solution)/shard_map/reshape | solution.py:63
  90.6 0.0 copy-start.1
  90.6 0.0 copy-start.3
  90.6 3.2 %convolution_bitcast_fusion = f32[2,32,64,64]{2,3,0,1:T(8,128)S(1)} fusion(f32[32,64,64,1]{1,2,3,0:T(8,128)} %copy.35, f32[1,64,64]{2,1,0:T(8,128)S(1)} %get-tuple-element.21, f32[1,64,64]{2,1,0:T(8,128)S(1)} %get-tuple-element.22), kind=kOutput, calls=%fused_computation.20 | convolution fusion | flops 201334784 | bytes 1605632 | tf_op jit(solution)/shard_map/pft,cts->pcfs/dot_general | solution.py:66
  93.8 0.0 copy-done.1
  93.8 0.0 copy-done.3
  93.8 1.0 multiply_subtract_fusion.3
  94.8 3.6 %fusion.15 = f32[2,32,64,64]{3,2,0,1:T(8,128)S(1)} fusion(f32[1,32,64,64]{2,3,0,1:T(8,128)S(1)} %get-tuple-element.10, f32[1,32,64,64]{2,3,0,1:T(8,128)S(1)} %get-tuple-element.9, f32[1,64,2,64]{3,1,2,0:T(8,128)S(1)} %get-tuple-element.14, f32[1,64,2,64]{3,1,2,0:T(8,128)S(1)} %get-tuple-element.19), kind=kOutput, calls=%fused_computation.19 | convolution fusion | flops 402931712 | bytes 2162688 | tf_op jit(solution)/shard_map/pgrs,rcfs->pcfg/dot_general | solution.py:68
  98.4 3.4 %fusion.14 = f32[2,32,64,64]{3,2,0,1:T(8,128)S(1)} fusion(f32[1,32,64,64]{2,3,0,1:T(8,128)S(1)} %get-tuple-element.17, f32[1,32,64,64]{2,3,0,1:T(8,128)S(1)} %get-tuple-element.18, f32[1,64,2,64]{3,1,2,0:T(8,128)S(1)} %get-tuple-element.14, f32[1,64,2,64]{3,1,2,0:T(8,128)S(1)} %get-tuple-element.19), kind=kOutput, calls=%fused_computation.18 | convolution fusion | flops 402931712 | bytes 2162688 | tf_op jit(solution)/shard_map/pgrs,rcfs->pcfg/dot_general | solution.py:68
  101.8 0.4 multiply_subtract_fusion.1
  102.3 3.5 %fusion.13 = f32[2,32,64,64]{2,3,0,1:T(8,128)S(1)} fusion(f32[1,32,64,64]{3,2,0,1:T(8,128)S(1)} %get-tuple-element.6, f32[1,32,64,64]{3,2,0,1:T(8,128)S(1)} %get-tuple-element.5, f32[1,64,2,64]{3,1,2,0:T(8,128)S(1)} %get-tuple-element.20, f32[1,64,2,64]{3,1,2,0:T(8,128)S(1)} %get-tuple-element.13), kind=kOutput, calls=%fused_computation.17 | convolution fusion | flops 402931712 | bytes 2162688 | tf_op jit(solution)/shard_map/pgrs,rcfs->pcfg/dot_general | solution.py:75
  105.8 0.3 multiply_subtract_fusion
  106.1 1.9 %fusion.22 = f32[32,64,64]{1,2,0:T(8,128)S(1)} fusion(f32[1,32,64,64]{2,3,0,1:T(8,128)S(1)} %get-tuple-element.8, f32[1,32,64,64]{2,3,0,1:T(8,128)S(1)} %get-tuple-element.7, f32[1,64,64]{2,1,0:T(8,128)S(1)} %get-tuple-element.21, f32[1,64,64]{2,1,0:T(8,128)S(1)} %get-tuple-element.22), kind=kOutput, calls=%fused_computation.24 | convolution fusion | flops 201728000 | bytes 1605632 | tf_op jit(solution)/shard_map/rft,rcfs->cts/dot_general | solution.py:77
  108.0 0.3 copy.28
  108.3 0.0 copy-start.2
  108.3 0.0 copy-start.5
  108.4 0.4 reshape.213
  108.7 0.7 copy.53
  109.5 4.0 %all-to-all-start.1 = ((f32[32,8,256]{2,0,1:T(8,128)}), f32[32,8,256]{2,0,1:T(8,128)S(1)}, u32[]{:S(2)}, u32[]{:S(2)}) async-start(f32[32,8,256]{2,0,1:T(8,128)} %bitcast.100), calls=%async_computation.1 | async-start | bytes 524288 | tf_op jit(solution)/shard_map/all_to_all | solution.py:103
  113.5 0.0 copy-done.2
  113.5 0.1 copy.31
  113.6 7.0 %all-to-all-done.1 = f32[32,8,256]{2,0,1:T(8,128)S(1)} async-done(((f32[32,8,256]{2,0,1:T(8,128)}), f32[32,8,256]{2,0,1:T(8,128)S(1)}, u32[]{:S(2)}, u32[]{:S(2)}) %all-to-all-start.1) | async-done | bytes 262176 | tf_op jit(solution)/shard_map/all_to_all | solution.py:103
  120.7 0.0 copy-done.5
  120.7 1.1 fusion.27
  121.7 9.6 %all_gather.7 = bf16[256,1024]{0,1:T(8,128)(2,1)S(1)} all-gather(bf16[256,256]{0,1:T(8,128)(2,1)S(1)} %fusion.27), channel_id=1, replica_groups=mesh['seq'=8,'ch'=4] {'ch'}, dimensions={1}, use_global_device_ids=true | all-gather | bytes 655360 | tf_op jit(solution)/shard_map/all_gather | solution.py:106
  131.4 0.0 copy-done
  131.4 1.3 fusion.65
  (4 shorter events, 0.1 us)
Async XLA Ops:
  6.5 124.8 %copy-start = (bf16[1024,512]{1,0:T(8,128)(2,1)S(1)}, bf16[1024,512]{1,0:T(8,128)(2,1)}, u32[]{:S(2)}) copy-start(bf16[1024,512]{1,0:T(8,128)(2,1)} %param.9) | copy-start | bytes 3145732
  6.5 77.6 %all-gather.2.cloned.1.call-start = ((), (), s32[]{:S(2)}) async-start(), calls=%async_computation.2 | async-start | bytes 4718592 | tf_op jit(solution)/shard_map/all_gather | solution.py:89
  9.0 13.8 %all-to-all-start = ((f32[8,32,256]{2,1,0:T(8,128)}), f32[8,32,256]{2,1,0:T(8,128)S(1)}, u32[]{:S(2)}, u32[]{:S(2)}) async-start(f32[8,32,256]{2,1,0:T(8,128)} %bitcast.1), calls=%async_computation | async-start | bytes 524288 | tf_op jit(solution)/shard_map/all_to_all | solution.py:92
  22.9 61.3 %copy-start.4 = (pred[4096]{0:T(1024)(128)(4,1)S(1)}, pred[4096]{0:T(1024)(128)(4,1)}, u32[]{:S(2)}) copy-start(pred[4096]{0:T(1024)(128)(4,1)} %constant.47.clone.1) | copy-start | bytes 12292
  90.6 3.2 %copy-start.1 = (f32[2,32,64,64]{2,3,0,1:T(8,128)S(1)}, f32[2,32,64,64]{2,3,0,1:T(8,128)}, u32[]{:S(2)}) copy-start(f32[2,32,64,64]{2,3,0,1:T(8,128)} %convolution_bitcast_fusion.1) | copy-start | bytes 3145732
  90.6 3.2 %copy-start.3 = (f32[64,64]{0,1:T(8,128)S(1)}, f32[64,64]{0,1:T(8,128)}, u32[]{:S(2)}) copy-start(f32[64,64]{0,1:T(8,128)} %get-tuple-element.24) | copy-start | bytes 49156
  108.3 5.2 %copy-start.2 = (f32[256,256]{1,0:T(8,128)S(1)}, f32[256,256]{1,0:T(8,128)}, u32[]{:S(2)}) copy-start(f32[256,256]{1,0:T(8,128)} %param.6) | copy-start | bytes 786436
  108.3 12.3 %copy-start.5 = (f32[256]{0:T(256)S(1)}, f32[256]{0:T(256)}, u32[]{:S(2)}) copy-start(f32[256]{0:T(256)} %param.8) | copy-start | bytes 3076
  109.5 11.2 %all-to-all-start.1 = ((f32[32,8,256]{2,0,1:T(8,128)}), f32[32,8,256]{2,0,1:T(8,128)S(1)}, u32[]{:S(2)}, u32[]{:S(2)}) async-start(f32[32,8,256]{2,0,1:T(8,128)} %bitcast.100), calls=%async_computation.1 | async-start | bytes 524288 | tf_op jit(solution)/shard_map/all_to_all | solution.py:103
Sparse Core Ops, SparseCore 0:
  9.5 74.6 all-gather.1
where the time goes:
time: 140 us; the launch traced here: 139 us
  waiting for transfers between devices  71.4 us (51%)
  matrix products  20.1 us (14%)
  between operations  13.6 us (10%)
  starting transfers between devices  10.4 us (7%)
  blocking collectives  9.63 us (7%)
  other arithmetic  8.11 us (6%)
  local copies, waits for them, and re-layouts  6.27 us (4%)
    all_gather x1, waiting for transfers between devices, body(): whole_filter = lax.all_gather(filter_taps, 'seq', axis=0, tiled=True)  57.6 us
    all_gather x1, blocking collectives, body(): lax.all_gather(hidden, 'ch', axis=1, tiled=True)  9.63 us
    dot_general x2, matrix products, forward_rows(): jnp.einsum('pgrs,rcfs->pcfg', tail_forward, twisted, precision=HIGHEST)  7.04 us
    all_to_all x1, waiting for transfers between devices, body(): lax.all_to_all(convolved_rows, 'seq', split_axis=1, concat_axis=0, tiled=...  7.02 us
    dot_general x2, matrix products, forward_rows(): section = jnp.einsum('pft,cts->pcfs', lead_table, signal, precision=HIGHEST)  6.41 us
    all_to_all x1, starting transfers between devices, body(): lax.all_to_all(values.T, 'seq', split_axis=0, concat_axis=1, tiled=True)  6.34 us
    all_to_all x1, waiting for transfers between devices, body(): lax.all_to_all(values.T, 'seq', split_axis=0, concat_axis=1, tiled=True)  6.05 us
    all_to_all x1, starting transfers between devices, body(): lax.all_to_all(convolved_rows, 'seq', split_axis=1, concat_axis=0, tiled=...  4.04 us
  transfers between devices with their start and end apart: 3, of which 3 were waited for; matrix products, arithmetic and copies ran while one was open for 5% of the time, Pallas kernels for 0%

commit v1 on v0

--- a/solution.py
+++ b/solution.py
@@ -1,11 +1,17 @@
+import functools
 import math
 
 import jax
 import jax.numpy as jnp
 from jax import lax
+from jax.experimental import pallas as pl
+from jax.experimental.pallas import tpu as pltpu
 from jax.sharding import PartitionSpec as P
 
 HIGHEST = lax.Precision.HIGHEST
+MESH = pl.DeviceIdType.MESH
+LANES = 128
+TILE = 16
 
 
 def split_length(length):
@@ -109,8 +115,263 @@
     )
 
 
+def toeplitz_kernel(
+    tap_sources,
+    values_ref,
+    gates_ref,
+    taps_ref,
+    skip_ref,
+    weight_ref,
+    out_ref,
+    x_out,
+    h_out,
+    x_in,
+    h_in,
+    x_rows,
+    toeplitz,
+    h_blocks,
+    y_blocks,
+    y_out,
+    y_in,
+    hidden,
+    weight,
+    weight_sem,
+    x_send,
+    x_recv,
+    h_send,
+    h_recv,
+    y_send,
+    y_recv,
+    g_send,
+    g_recv,
+):
+    seq_size, narrow, block_rows = x_out.shape
+    tap_rows = h_out.shape[2]
+    ch_size, _, width = hidden.shape
+    blocks = x_rows.shape[0] // narrow
+    per = block_rows // LANES
+    groups = narrow // TILE
+    me, lane_group = lax.axis_index("seq"), lax.axis_index("ch")
+    f32, bf16 = jnp.float32, jnp.bfloat16
+
+    weight_copy = pltpu.make_async_copy(weight_ref, weight, weight_sem)
+    weight_copy.start()
+
+    barrier = pltpu.get_barrier_semaphore()
+    for step in range(1, seq_size):
+        pl.semaphore_signal(
+            barrier, inc=1, device_id={"seq": lax.rem(me + step, seq_size)}, device_id_type=MESH
+        )
+    for step in range(1, ch_size):
+        pl.semaphore_signal(
+            barrier, inc=1, device_id={"ch": lax.rem(lane_group + step, ch_size)}, device_id_type=MESH
+        )
+
+    x_out[...] = values_ref[...].T.astype(bf16).reshape(x_out.shape)
+
+    @pl.when(me < tap_sources)
+    def _():
+        h_out[...] = taps_ref[...].T.astype(bf16).reshape(h_out.shape)
+
+    h_blocks[...] = jnp.zeros_like(h_blocks)
+    pl.semaphore_wait(barrier, seq_size + ch_size - 2)
+
+    x_copies = []
+    for step in range(1, seq_size):
+        to = lax.rem(me + step, seq_size)
+        copy = pltpu.make_async_remote_copy(
+            x_out.at[to], x_in.at[me], x_send.at[step], x_recv.at[step],
+            device_id={"seq": to}, device_id_type=MESH,
+        )
+        copy.start()
+        x_copies.append(copy)
+
+    def tap_copy(step):
+        to = lax.rem(me + step, seq_size)
+        return pltpu.make_async_remote_copy(
+            h_out.at[to], h_in.at[me], h_send.at[step], h_recv.at[me],
+            device_id={"seq": to}, device_id_type=MESH,
+        )
+
+    @pl.when(me < tap_sources)
+    def _():
+        for step in range(1, seq_size):
+            tap_copy(step).start()
+        h_in[me] = h_out[me]
+
+    x_in[me] = x_out[me]
+    for copy in x_copies:
+        copy.wait_recv()
+    for source in range(seq_size):
+        for piece in range(per):
+            x_rows[pl.ds(source * per + piece, narrow, stride=blocks), :] = x_in[
+                source, :, piece * LANES : (piece + 1) * LANES
+            ].astype(f32)
+
+    row_ids = lax.broadcasted_iota(jnp.int32, (LANES, LANES), 0)
+    col_ids = lax.broadcasted_iota(jnp.int32, (LANES, LANES), 1)
+
+    def build(channel, carry):
+        before = jnp.zeros((LANES, LANES), f32)
+        rows = x_rows[pl.ds(pl.multiple_of(channel * blocks, blocks), blocks), :]
+        for block in range(blocks):
+            row = rows[block : block + 1]
+            turned = pltpu.roll(
+                jnp.broadcast_to(row, (LANES, LANES)), 0, 1, stride=1, stride_axis=0
+            )
+            toeplitz[channel, block * LANES : (block + 1) * LANES, :] = jnp.where(
+                col_ids >= row_ids, turned, before
+            ).astype(bf16)
+            before = turned
+        return carry
+
+    lax.fori_loop(0, narrow, build, 0)
+
+    for source in range(tap_sources):
+        @pl.when(me != source)
+        def _():
+            pltpu.make_async_remote_copy(
+                h_out.at[0], h_in.at[source], h_send.at[0], h_recv.at[source],
+                device_id={"seq": source}, device_id_type=MESH,
+            ).wait_recv()
+
+    pieces = tap_rows // LANES
+    flat_blocks = h_blocks.reshape(narrow * 2 * blocks, LANES)
+    for source in range(tap_sources):
+        for piece in range(pieces):
+            flat_blocks[pl.ds(blocks + source * pieces + piece, narrow, stride=2 * blocks), :] = h_in[
+                source, :, piece * LANES : (piece + 1) * LANES
+            ].astype(f32)
+
+    def convolve(channel, carry):
+        left = jnp.concatenate(
+            [h_blocks[channel, blocks - lag : 2 * blocks - lag, :] for lag in range(blocks)], axis=1
+        ).astype(bf16)
+        y_blocks[pl.ds(pl.multiple_of(channel * blocks, blocks), blocks), :] = jnp.dot(
+            left, toeplitz[channel], preferred_element_type=f32
+        )
+        return carry
+
+    y_copies = []
+    for group in range(groups):
+        lax.fori_loop(group * TILE, (group + 1) * TILE, convolve, 0)
+        rows = slice(group * TILE, (group + 1) * TILE)
+        for block in range(blocks):
+            y_out[block // per, rows, (block % per) * LANES : (block % per + 1) * LANES] = y_blocks[
+                pl.ds(group * TILE * blocks + block, TILE, stride=blocks), :
+            ].astype(bf16)
+        for step in range(1, seq_size):
+            to = lax.rem(me + step, seq_size)
+            copy = pltpu.make_async_remote_copy(
+                y_out.at[to, rows], y_in.at[me, rows], y_send.at[group, step], y_recv.at[group, step],
+                device_id={"seq": to}, device_id_type=MESH,
+            )
+            copy.start()
+            y_copies.append(copy)
+    y_in[me] = y_out[me]
+    for copy in y_copies:
+        copy.wait_recv()
+
+    convolved = y_in[...].astype(f32).reshape(width, block_rows).T
+    gated = (gates_ref[...] * (convolved + skip_ref[...] * values_ref[...])).astype(bf16)
+    hidden[lane_group] = gated
+
+    g_copies = []
+    for step in range(1, ch_size):
+        copy = pltpu.make_async_remote_copy(
+            hidden.at[lane_group], hidden.at[lane_group], g_send.at[step], g_recv.at[step],
+            device_id={"ch": lax.rem(lane_group + step, ch_size)}, device_id_type=MESH,
+        )
+        copy.start()
+        g_copies.append(copy)
+    weight_copy.wait()
+    out_ref[...] = jnp.dot(gated, weight[lane_group], preferred_element_type=f32)
+    for step in range(1, ch_size):
+        source = lax.rem(lane_group + ch_size - step, ch_size)
+        g_copies[step - 1].wait_recv()
+        out_ref[...] += jnp.dot(hidden[source], weight[source], preferred_element_type=f32)
+
+    for copy in x_copies + y_copies + g_copies:
+        copy.wait_send()
+
+    @pl.when(me < tap_sources)
+    def _():
+        for step in range(1, seq_size):
+            tap_copy(step).wait_send()
+
+
+def toeplitz_body(values, gates, filter_taps, skip, out_weight):
+    seq_size, ch_size = lax.axis_size("seq"), lax.axis_size("ch")
+    block_rows, width = values.shape
+    tap_rows = filter_taps.shape[0]
+    narrow = width // seq_size
+    total = block_rows * seq_size
+    sources = min(tap_rows * seq_size, total) // tap_rows
+    columns = out_weight.shape[1]
+    f32, bf16 = jnp.float32, jnp.bfloat16
+    vmem = pl.BlockSpec(memory_space=pltpu.VMEM)
+    dma = pltpu.SemaphoreType.DMA
+    return pl.pallas_call(
+        functools.partial(toeplitz_kernel, sources),
+        out_shape=jax.ShapeDtypeStruct((block_rows, columns), f32),
+        in_specs=[vmem] * 4 + [pl.BlockSpec(memory_space=pl.ANY)],
+        out_specs=vmem,
+        scratch_shapes=[
+            pltpu.VMEM((seq_size, narrow, block_rows), bf16),
+            pltpu.VMEM((seq_size, narrow, tap_rows), bf16),
+            pltpu.VMEM((seq_size, narrow, block_rows), bf16),
+            pltpu.VMEM((sources, narrow, tap_rows), bf16),
+            pltpu.VMEM((narrow * (total // LANES), LANES), f32),
+            pltpu.VMEM((narrow, total, LANES), bf16),
+            pltpu.VMEM((narrow, 2 * (total // LANES), LANES), f32),
+            pltpu.VMEM((narrow * (total // LANES), LANES), f32),
+            pltpu.VMEM((seq_size, narrow, block_rows), bf16),
+            pltpu.VMEM((seq_size, narrow, block_rows), bf16),
+            pltpu.VMEM((ch_size, block_rows, width), bf16),
+            pltpu.VMEM((ch_size, width, columns), bf16),
+            dma(()),
+            dma((seq_size,)),
+            dma((seq_size,)),
+            dma((seq_size,)),
+            dma((sources,)),
+            dma((narrow // TILE, seq_size)),
+            dma((narrow // TILE, seq_size)),
+            dma((ch_size,)),
+            dma((ch_size,)),
+        ],
+        compiler_params=pltpu.CompilerParams(
+            collective_id=0, has_side_effects=True, vmem_limit_bytes=48 * 1024 * 1024
+        ),
+    )(
+        values,
+        gates,
+        filter_taps,
+        skip.reshape(1, width),
+        out_weight.reshape(ch_size, width, columns),
+    )
+
+
+def local_body(values, gates, filter_taps, skip, out_weight):
+    seq_size = lax.axis_size("seq")
+    block_rows, width = values.shape
+    tap_rows = filter_taps.shape[0]
+    narrow = width // seq_size
+    total = block_rows * seq_size
+    fits = (
+        width % (seq_size * TILE) == 0
+        and width % LANES == 0
+        and block_rows % LANES == 0
+        and total // LANES % 8 == 0
+        and tap_rows % LANES == 0
+        and total % tap_rows == 0
+        and narrow * total * LANES * 2 <= 32 * 1024 * 1024
+    )
+    chosen = toeplitz_body if fits else body
+    return chosen(values, gates, filter_taps, skip, out_weight)
+
+
 def solution(mesh):
     placed = (P("seq", "ch"), P("seq", "ch"), P("seq", "ch"), P("ch"), P(None, "ch"))
     return jax.shard_map(
-        body, mesh=mesh, in_specs=placed, out_specs=P("seq", "ch"), check_vma=False
-    )
+        local_body, mesh=mesh, in_specs=placed, out_specs=P("seq", "ch"), check_vma=False
+    )

time: 140 us -> 41.8 us (0.30)
  waiting for transfers between devices: 71.4 us -> 0 us
  Pallas kernels: 0 us -> 35.9 us
  matrix products: 20.1 us -> 0 us
  between operations: 13.6 us -> 0.01 us
  starting transfers between devices: 10.4 us -> 0 us
  blocking collectives: 9.63 us -> 0 us
  other arithmetic: 8.11 us -> 0 us
    all_gather x1 -> x0, waiting for transfers between devices: 57.6 us -> none  [body(): whole_filter = lax.all_gather(filter_taps, 'seq', axis=0, tiled=True)]
    pallas_call x0 -> x1, Pallas kernels: none -> 35.9 us  [toeplitz_body(): pl.pallas_call(functools.partial(toeplitz_kernel, sources), out_shape=jax...]
    dot_general x7 -> x0, matrix products: 20.1 us -> none  [the longest x2 7.04 us: forward_rows(): jnp.einsum('pgrs,rcfs->pcfg', tail_forward, twisted, precision=HIGHEST)]
    all_to_all x2 -> x0, waiting for transfers between devices: 13.1 us -> none  [the longest x1 7.02 us: body(): lax.all_to_all(convolved_rows, 'seq', split_axis=1, concat_axis=0, tiled=...]
    all_to_all x2 -> x0, starting transfers between devices: 10.4 us -> none  [the longest x1 6.34 us: body(): lax.all_to_all(values.T, 'seq', split_axis=0, concat_axis=1, tiled=True)]
    all_gather x1 -> x0, blocking collectives: 9.63 us -> none  [body(): lax.all_gather(hidden, 'ch', axis=1, tiled=True)]
    concatenate x1 -> x0, other arithmetic: 3.95 us -> none  [forward_rows(): jnp.concatenate([rows, jnp.zeros_like(rows)], axis=1)]
    unnamed x14 -> x11, local copies, waits for them, and re-layouts: 1.95 us -> 5.64 us
  transfers between devices with their start and end apart: 3 -> 0, of which waited for: 3 -> 0; matrix products, arithmetic and copies ran while one was open for 5% -> 0% of each run, Pallas kernels for 0% -> 0%
where the time goes in v1:
time: 41.8 us; the launch traced here: 41.5 us
  Pallas kernels  35.9 us (86%)
  local copies, waits for them, and re-layouts  5.64 us (13%)
    pallas_call x1, Pallas kernels, toeplitz_body(): pl.pallas_call(functools.partial(toeplitz_kernel, sources), out_shape=jax...  35.9 us
    unnamed x11, local copies, waits for them, and re-layouts  5.64 us

profile of v1, /device:TPU:1, one launch (start us, length us, event | category | flops | bytes accessed | tf_op | source)
XLA Modules:
  0.0 41.5 jit_solution(13369387553730229170)
XLA Ops:
  0.0 0.0 copy-start.4
  0.0 0.7 %copy-done.4 = f32[256]{0:T(256)S(1)} copy-done((f32[256]{0:T(256)S(1)}, f32[256]{0:T(256)}, u32[]{:S(2)}) %copy-start.4) | copy-done | bytes 1048
  0.7 0.0 copy-start
  0.7 1.2 %copy-done = bf16[1024,512]{1,0:T(8,128)(2,1)S(1)} copy-done((bf16[1024,512]{1,0:T(8,128)(2,1)S(1)}, bf16[1024,512]{1,0:T(8,128)(2,1)}, u32[]{:S(2)}) %copy-start) | copy-done | bytes 1048600
  1.9 0.0 copy-start.1
  1.9 1.0 %copy-done.1 = f32[512,256]{1,0:T(8,128)S(1)} copy-done((f32[512,256]{1,0:T(8,128)S(1)}, f32[512,256]{1,0:T(8,128)}, u32[]{:S(2)}) %copy-start.1) | copy-done | bytes 524312
  2.9 0.0 copy-start.2
  2.9 0.9 %copy-done.2 = f32[256,256]{1,0:T(8,128)S(1)} copy-done((f32[256,256]{1,0:T(8,128)S(1)}, f32[256,256]{1,0:T(8,128)}, u32[]{:S(2)}) %copy-start.2) | copy-done | bytes 262168
  3.9 0.0 copy-start.3
  3.9 0.9 %copy-done.3 = f32[256,256]{1,0:T(8,128)S(1)} copy-done((f32[256,256]{1,0:T(8,128)S(1)}, f32[256,256]{1,0:T(8,128)}, u32[]{:S(2)}) %copy-start.3) | copy-done | bytes 262168
  4.8 35.9 %shard_map.55 = f32[256,512]{1,0:T(8,128)S(1)} custom-call(f32[256,256]{1,0:T(8,128)S(1)} %copy-done.2, f32[256,256]{1,0:T(8,128)S(1)} %copy-done.3, f32[512,256]{1,0:T(8,128)S(1)} %copy-done.1, f32[1,256]{1,0:T(1,128)S(1)} %bitcast.3, bf16[4,256,512]{2,1,0:T(8,128)(2,1)S(1)} %bitcast.2), custom_call_target="tpu_custom_call" | custom-call | tf_op jit(solution)/shard_map/pallas_call | solution.py:314
  40.8 0.8 %copy.7 = f32[256,512]{1,0:T(8,128)} copy(f32[256,512]{1,0:T(8,128)S(1)} %shard_map.55) | data formatting | bytes 1048576
Async XLA Ops:
  0.0 0.7 %copy-start.4 = (f32[256]{0:T(256)S(1)}, f32[256]{0:T(256)}, u32[]{:S(2)}) copy-start(f32[256]{0:T(256)} %param.8) | copy-start | bytes 3076
  0.7 1.2 %copy-start = (bf16[1024,512]{1,0:T(8,128)(2,1)S(1)}, bf16[1024,512]{1,0:T(8,128)(2,1)}, u32[]{:S(2)}) copy-start(bf16[1024,512]{1,0:T(8,128)(2,1)} %param.9) | copy-start | bytes 3145732
  1.9 1.0 %copy-start.1 = (f32[512,256]{1,0:T(8,128)S(1)}, f32[512,256]{1,0:T(8,128)}, u32[]{:S(2)}) copy-start(f32[512,256]{1,0:T(8,128)} %taps_ref.1) | copy-start | bytes 1572868
  2.9 0.9 %copy-start.2 = (f32[256,256]{1,0:T(8,128)S(1)}, f32[256,256]{1,0:T(8,128)}, u32[]{:S(2)}) copy-start(f32[256,256]{1,0:T(8,128)} %values_ref.1) | copy-start | bytes 786436
  3.9 0.9 %copy-start.3 = (f32[256,256]{1,0:T(8,128)S(1)}, f32[256,256]{1,0:T(8,128)}, u32[]{:S(2)}) copy-start(f32[256,256]{1,0:T(8,128)} %gates_ref.1) | copy-start | bytes 786436

commit v2 on v1

--- a/solution.py
+++ b/solution.py
@@ -12,6 +12,8 @@
 MESH = pl.DeviceIdType.MESH
 LANES = 128
 TILE = 16
+BUILD_UNROLL = 2
+CONV_UNROLL = 4
 
 
 def split_length(length):
@@ -117,11 +119,15 @@
 
 def toeplitz_kernel(
     tap_sources,
+    values_hbm,
+    gates_hbm,
+    taps_hbm,
+    skip_ref,
+    weight_hbm,
+    out_hbm,
     values_ref,
     gates_ref,
     taps_ref,
-    skip_ref,
-    weight_ref,
     out_ref,
     x_out,
     h_out,
@@ -135,7 +141,8 @@
     y_in,
     hidden,
     weight,
-    weight_sem,
+    load_sem,
+    out_sem,
     x_send,
     x_recv,
     h_send,
@@ -154,8 +161,19 @@
     me, lane_group = lax.axis_index("seq"), lax.axis_index("ch")
     f32, bf16 = jnp.float32, jnp.bfloat16
 
-    weight_copy = pltpu.make_async_copy(weight_ref, weight, weight_sem)
-    weight_copy.start()
+    loads = [
+        pltpu.make_async_copy(source, target, load_sem.at[place])
+        for place, (source, target) in enumerate(
+            (
+                (values_hbm, values_ref),
+                (taps_hbm, taps_ref),
+                (gates_hbm, gates_ref),
+                (weight_hbm, weight),
+            )
+        )
+    ]
+    for load in loads:
+        load.start()
 
     barrier = pltpu.get_barrier_semaphore()
     for step in range(1, seq_size):
@@ -167,13 +185,9 @@
             barrier, inc=1, device_id={"ch": lax.rem(lane_group + step, ch_size)}, device_id_type=MESH
         )
 
+    h_blocks[...] = jnp.zeros_like(h_blocks)
+    loads[0].wait()
     x_out[...] = values_ref[...].T.astype(bf16).reshape(x_out.shape)
-
-    @pl.when(me < tap_sources)
-    def _():
-        h_out[...] = taps_ref[...].T.astype(bf16).reshape(h_out.shape)
-
-    h_blocks[...] = jnp.zeros_like(h_blocks)
     pl.semaphore_wait(barrier, seq_size + ch_size - 2)
 
     x_copies = []
@@ -186,6 +200,8 @@
         copy.start()
         x_copies.append(copy)
 
+    loads[1].wait()
+
     def tap_copy(step):
         to = lax.rem(me + step, seq_size)
         return pltpu.make_async_remote_copy(
@@ -195,6 +211,7 @@
 
     @pl.when(me < tap_sources)
     def _():
+        h_out[...] = taps_ref[...].T.astype(bf16).reshape(h_out.shape)
         for step in range(1, seq_size):
             tap_copy(step).start()
         h_in[me] = h_out[me]
@@ -211,7 +228,7 @@
     row_ids = lax.broadcasted_iota(jnp.int32, (LANES, LANES), 0)
     col_ids = lax.broadcasted_iota(jnp.int32, (LANES, LANES), 1)
 
-    def build(channel, carry):
+    def build_one(channel):
         before = jnp.zeros((LANES, LANES), f32)
         rows = x_rows[pl.ds(pl.multiple_of(channel * blocks, blocks), blocks), :]
         for block in range(blocks):
@@ -223,9 +240,13 @@
                 col_ids >= row_ids, turned, before
             ).astype(bf16)
             before = turned
+
+    def build(turn, carry):
+        for part in range(BUILD_UNROLL):
+            build_one(turn * BUILD_UNROLL + part)
         return carry
 
-    lax.fori_loop(0, narrow, build, 0)
+    lax.fori_loop(0, narrow // BUILD_UNROLL, build, 0)
 
     for source in range(tap_sources):
         @pl.when(me != source)
@@ -243,18 +264,23 @@
                 source, :, piece * LANES : (piece + 1) * LANES
             ].astype(f32)
 
-    def convolve(channel, carry):
+    def convolve_one(channel):
         left = jnp.concatenate(
             [h_blocks[channel, blocks - lag : 2 * blocks - lag, :] for lag in range(blocks)], axis=1
         ).astype(bf16)
         y_blocks[pl.ds(pl.multiple_of(channel * blocks, blocks), blocks), :] = jnp.dot(
             left, toeplitz[channel], preferred_element_type=f32
         )
+
+    def convolve(turn, carry):
+        for part in range(CONV_UNROLL):
+            convolve_one(turn * CONV_UNROLL + part)
         return carry
 
     y_copies = []
     for group in range(groups):
-        lax.fori_loop(group * TILE, (group + 1) * TILE, convolve, 0)
+        turns = TILE // CONV_UNROLL
+        lax.fori_loop(group * turns, (group + 1) * turns, convolve, 0)
         rows = slice(group * TILE, (group + 1) * TILE)
         for block in range(blocks):
             y_out[block // per, rows, (block % per) * LANES : (block % per + 1) * LANES] = y_blocks[
@@ -272,24 +298,61 @@
     for copy in y_copies:
         copy.wait_recv()
 
-    convolved = y_in[...].astype(f32).reshape(width, block_rows).T
-    gated = (gates_ref[...] * (convolved + skip_ref[...] * values_ref[...])).astype(bf16)
-    hidden[lane_group] = gated
-
-    g_copies = []
-    for step in range(1, ch_size):
+    partner = lane_group + 1 - 2 * lax.rem(lane_group, 2)
+    pairs = ch_size // 2
+
+    def spread(kind, piece, slot, to):
+        block = hidden.at[slot, pl.ds(piece * LANES, LANES)]
         copy = pltpu.make_async_remote_copy(
-            hidden.at[lane_group], hidden.at[lane_group], g_send.at[step], g_recv.at[step],
-            device_id={"ch": lax.rem(lane_group + step, ch_size)}, device_id_type=MESH,
+            block, block, g_send.at[kind, piece], g_recv.at[kind, piece],
+            device_id={"ch": to}, device_id_type=MESH,
         )
         copy.start()
         g_copies.append(copy)
-    weight_copy.wait()
-    out_ref[...] = jnp.dot(gated, weight[lane_group], preferred_element_type=f32)
-    for step in range(1, ch_size):
-        source = lax.rem(lane_group + ch_size - step, ch_size)
-        g_copies[step - 1].wait_recv()
-        out_ref[...] += jnp.dot(hidden[source], weight[source], preferred_element_type=f32)
+        return copy
+
+    def add_product(piece, slot, first=False):
+        rows = slice(piece * LANES, (piece + 1) * LANES)
+        term = jnp.dot(hidden[slot, rows], weight[slot], preferred_element_type=f32)
+        out_ref[rows] = term if first else out_ref[rows] + term
+
+    g_copies, direct, relayed = [], {}, {}
+    loads[2].wait()
+    for piece in range(per):
+        rows = slice(piece * LANES, (piece + 1) * LANES)
+        convolved = y_in[:, :, rows].astype(f32).reshape(width, LANES).T
+        hidden[lane_group, rows] = (
+            gates_ref[rows] * (convolved + skip_ref[...] * values_ref[rows])
+        ).astype(bf16)
+        for pair in range(1, pairs):
+            direct[pair, piece] = spread(
+                2 * pair - 1, piece, lane_group, lax.rem(lane_group + 2 * pair, ch_size)
+            )
+        direct[0, piece] = spread(0, piece, lane_group, partner)
+    loads[3].wait()
+    for piece in range(per):
+        add_product(piece, lane_group, True)
+    for piece in range(per):
+        direct[0, piece].wait_recv()
+        add_product(piece, partner)
+    for piece in range(per):
+        for pair in range(1, pairs):
+            slot = lax.rem(lane_group + ch_size - 2 * pair, ch_size)
+            direct[pair, piece].wait_recv()
+            relayed[pair, piece] = spread(2 * pair, piece, slot, partner)
+            add_product(piece, slot)
+    stores = []
+    for piece in range(per):
+        rows = pl.ds(piece * LANES, LANES)
+        for pair in range(1, pairs):
+            slot = lax.rem(partner + ch_size - 2 * pair, ch_size)
+            relayed[pair, piece].wait_recv()
+            add_product(piece, slot)
+        store = pltpu.make_async_copy(out_ref.at[rows], out_hbm.at[rows], out_sem.at[piece])
+        store.start()
+        stores.append(store)
+    for store in stores:
+        store.wait()
 
     for copy in x_copies + y_copies + g_copies:
         copy.wait_send()
@@ -310,13 +373,19 @@
     columns = out_weight.shape[1]
     f32, bf16 = jnp.float32, jnp.bfloat16
     vmem = pl.BlockSpec(memory_space=pltpu.VMEM)
+    hbm = pl.BlockSpec(memory_space=pl.ANY)
+    per = block_rows // LANES
     dma = pltpu.SemaphoreType.DMA
     return pl.pallas_call(
         functools.partial(toeplitz_kernel, sources),
         out_shape=jax.ShapeDtypeStruct((block_rows, columns), f32),
-        in_specs=[vmem] * 4 + [pl.BlockSpec(memory_space=pl.ANY)],
-        out_specs=vmem,
+        in_specs=[hbm] * 3 + [vmem, hbm],
+        out_specs=hbm,
         scratch_shapes=[
+            pltpu.VMEM((block_rows, width), f32),
+            pltpu.VMEM((block_rows, width), f32),
+            pltpu.VMEM((tap_rows, width), f32),
+            pltpu.VMEM((block_rows, columns), f32),
             pltpu.VMEM((seq_size, narrow, block_rows), bf16),
             pltpu.VMEM((seq_size, narrow, tap_rows), bf16),
             pltpu.VMEM((seq_size, narrow, block_rows), bf16),
@@ -329,18 +398,19 @@
             pltpu.VMEM((seq_size, narrow, block_rows), bf16),
             pltpu.VMEM((ch_size, block_rows, width), bf16),
             pltpu.VMEM((ch_size, width, columns), bf16),
-            dma(()),
+            dma((4,)),
+            dma((per,)),
             dma((seq_size,)),
             dma((seq_size,)),
             dma((seq_size,)),
             dma((sources,)),
             dma((narrow // TILE, seq_size)),
             dma((narrow // TILE, seq_size)),
-            dma((ch_size,)),
-            dma((ch_size,)),
+            dma((ch_size, per)),
+            dma((ch_size, per)),
         ],
         compiler_params=pltpu.CompilerParams(
-            collective_id=0, has_side_effects=True, vmem_limit_bytes=48 * 1024 * 1024
+            collective_id=0, has_side_effects=True, vmem_limit_bytes=63000 * 1024
         ),
     )(
         values,
@@ -359,6 +429,7 @@
     total = block_rows * seq_size
     fits = (
         width % (seq_size * TILE) == 0
+        and lax.axis_size("ch") % 2 == 0
         and width % LANES == 0
         and block_rows % LANES == 0
         and total // LANES % 8 == 0

time: 41.8 us -> 35.4 us (0.85)
  local copies, waits for them, and re-layouts: 5.64 us -> 1.87 us
  Pallas kernels: 35.9 us -> 33.3 us
    unnamed x11 -> x1, local copies, waits for them, and re-layouts: 5.64 us -> 1.87 us
    pallas_call x1, Pallas kernels: 35.9 us -> 33.3 us  [toeplitz_body(): pl.pallas_call(functools.partial(toeplitz_kernel, sources), out_shape=jax...]
where the time goes in v2:
time: 35.4 us; the launch traced here: 35.2 us
  Pallas kernels  33.3 us (94%)
  local copies, waits for them, and re-layouts  1.87 us (5%)
    pallas_call x1, Pallas kernels, toeplitz_body(): pl.pallas_call(functools.partial(toeplitz_kernel, sources), out_shape=jax...  33.3 us
    unnamed x1, local copies, waits for them, and re-layouts  1.87 us

profile of v2, /device:TPU:1, one launch (start us, length us, event | category | flops | bytes accessed | tf_op | source)
XLA Modules:
  0.0 35.2 jit_solution(2680352192280582451)
XLA Ops:
  0.0 33.3 %shard_map.55 = f32[256,512]{1,0:T(8,128)} custom-call(f32[256,256]{1,0:T(8,128)} %values_hbm.1, f32[256,256]{1,0:T(8,128)} %gates_hbm.1, f32[512,256]{1,0:T(8,128)} %taps_hbm.1, f32[1,256]{1,0:T(1,128)} %bitcast.3, bf16[4,256,512]{2,1,0:T(8,128)(2,1)} %bitcast.2), custom_call_target="tpu_custom_call" | custom-call | tf_op jit(solution)/shard_map/pallas_call | solution.py:379
  33.3 1.9 %copy.7 = f32[256,512]{1,0:T(8,128)} copy(f32[256,512]{1,0:T(8,128)} %shard_map.55) | data formatting | bytes 1048576

commit v3 on v2

--- a/solution.py
+++ b/solution.py
@@ -12,8 +12,8 @@
 MESH = pl.DeviceIdType.MESH
 LANES = 128
 TILE = 16
-BUILD_UNROLL = 2
-CONV_UNROLL = 4
+BUILD_UNROLL = 8
+CONV_UNROLL = 16
 
 
 def split_length(length):
@@ -157,7 +157,6 @@
     ch_size, _, width = hidden.shape
     blocks = x_rows.shape[0] // narrow
     per = block_rows // LANES
-    groups = narrow // TILE
     me, lane_group = lax.axis_index("seq"), lax.axis_index("ch")
     f32, bf16 = jnp.float32, jnp.bfloat16
 
@@ -190,15 +189,19 @@
     x_out[...] = values_ref[...].T.astype(bf16).reshape(x_out.shape)
     pl.semaphore_wait(barrier, seq_size + ch_size - 2)
 
+    groups = narrow // TILE
     x_copies = []
-    for step in range(1, seq_size):
-        to = lax.rem(me + step, seq_size)
-        copy = pltpu.make_async_remote_copy(
-            x_out.at[to], x_in.at[me], x_send.at[step], x_recv.at[step],
-            device_id={"seq": to}, device_id_type=MESH,
-        )
-        copy.start()
-        x_copies.append(copy)
+    for group in range(groups):
+        part = pl.ds(group * TILE, TILE)
+        for step in range(1, seq_size):
+            to = lax.rem(me + step, seq_size)
+            copy = pltpu.make_async_remote_copy(
+                x_out.at[to, part], x_in.at[me, part],
+                x_send.at[group, step], x_recv.at[group, step],
+                device_id={"seq": to}, device_id_type=MESH,
+            )
+            copy.start()
+            x_copies.append(copy)
 
     loads[1].wait()
 
@@ -217,14 +220,6 @@
         h_in[me] = h_out[me]
 
     x_in[me] = x_out[me]
-    for copy in x_copies:
-        copy.wait_recv()
-    for source in range(seq_size):
-        for piece in range(per):
-            x_rows[pl.ds(source * per + piece, narrow, stride=blocks), :] = x_in[
-                source, :, piece * LANES : (piece + 1) * LANES
-            ].astype(f32)
-
     row_ids = lax.broadcasted_iota(jnp.int32, (LANES, LANES), 0)
     col_ids = lax.broadcasted_iota(jnp.int32, (LANES, LANES), 1)
 
@@ -246,7 +241,16 @@
             build_one(turn * BUILD_UNROLL + part)
         return carry
 
-    lax.fori_loop(0, narrow // BUILD_UNROLL, build, 0)
+    turns = TILE // BUILD_UNROLL
+    for group in range(groups):
+        for copy in x_copies[group * (seq_size - 1) : (group + 1) * (seq_size - 1)]:
+            copy.wait_recv()
+        for source in range(seq_size):
+            for piece in range(per):
+                x_rows[pl.ds(group * TILE * blocks + source * per + piece, TILE, stride=blocks), :] = x_in[
+                    source, group * TILE : (group + 1) * TILE, piece * LANES : (piece + 1) * LANES
+                ].astype(f32)
+        lax.fori_loop(group * turns, (group + 1) * turns, build, 0)
 
     for source in range(tap_sources):
         @pl.when(me != source)
@@ -277,26 +281,23 @@
             convolve_one(turn * CONV_UNROLL + part)
         return carry
 
-    y_copies = []
-    for group in range(groups):
-        turns = TILE // CONV_UNROLL
-        lax.fori_loop(group * turns, (group + 1) * turns, convolve, 0)
-        rows = slice(group * TILE, (group + 1) * TILE)
-        for block in range(blocks):
-            y_out[block // per, rows, (block % per) * LANES : (block % per + 1) * LANES] = y_blocks[
-                pl.ds(group * TILE * blocks + block, TILE, stride=blocks), :
-            ].astype(bf16)
+    lax.fori_loop(0, narrow // CONV_UNROLL, convolve, 0)
+    for block in range(blocks):
+        y_out[block // per, :, (block % per) * LANES : (block % per + 1) * LANES] = y_blocks[
+            pl.ds(block, narrow, stride=blocks), :
+        ].astype(bf16)
+    y_copies = {}
+    for piece in range(per):
+        span = pl.ds(piece * LANES, LANES)
         for step in range(1, seq_size):
             to = lax.rem(me + step, seq_size)
-            copy = pltpu.make_async_remote_copy(
-                y_out.at[to, rows], y_in.at[me, rows], y_send.at[group, step], y_recv.at[group, step],
+            y_copies[piece, step] = pltpu.make_async_remote_copy(
+                y_out.at[to, :, span], y_in.at[me, :, span],
+                y_send.at[piece, step], y_recv.at[piece, step],
                 device_id={"seq": to}, device_id_type=MESH,
             )
-            copy.start()
-            y_copies.append(copy)
+            y_copies[piece, step].start()
     y_in[me] = y_out[me]
-    for copy in y_copies:
-        copy.wait_recv()
 
     partner = lane_group + 1 - 2 * lax.rem(lane_group, 2)
     pairs = ch_size // 2
@@ -320,6 +321,8 @@
     loads[2].wait()
     for piece in range(per):
         rows = slice(piece * LANES, (piece + 1) * LANES)
+        for step in range(1, seq_size):
+            y_copies[piece, step].wait_recv()
         convolved = y_in[:, :, rows].astype(f32).reshape(width, LANES).T
         hidden[lane_group, rows] = (
             gates_ref[rows] * (convolved + skip_ref[...] * values_ref[rows])
@@ -354,7 +357,7 @@
     for store in stores:
         store.wait()
 
-    for copy in x_copies + y_copies + g_copies:
+    for copy in x_copies + list(y_copies.values()) + g_copies:
         copy.wait_send()
 
     @pl.when(me < tap_sources)
@@ -400,12 +403,12 @@
             pltpu.VMEM((ch_size, width, columns), bf16),
             dma((4,)),
             dma((per,)),
-            dma((seq_size,)),
-            dma((seq_size,)),
+            dma((narrow // TILE, seq_size)),
+            dma((narrow // TILE, seq_size)),
             dma((seq_size,)),
             dma((sources,)),
-            dma((narrow // TILE, seq_size)),
-            dma((narrow // TILE, seq_size)),
+            dma((per, seq_size)),
+            dma((per, seq_size)),
             dma((ch_size, per)),
             dma((ch_size, per)),
         ],

time: 35.4 us -> 33 us (0.932)
  Pallas kernels: 33.3 us -> 30.9 us
    pallas_call x1, Pallas kernels: 33.3 us -> 30.9 us  [toeplitz_body(): pl.pallas_call(functools.partial(toeplitz_kernel, sources), out_shape=jax...]
where the time goes in v3:
time: 33 us; the launch traced here: 32.8 us
  Pallas kernels  30.9 us (94%)
  local copies, waits for them, and re-layouts  1.87 us (6%)
    pallas_call x1, Pallas kernels, toeplitz_body(): pl.pallas_call(functools.partial(toeplitz_kernel, sources), out_shape=jax...  30.9 us
    unnamed x1, local copies, waits for them, and re-layouts  1.87 us

profile of v3, /device:TPU:1, one launch (start us, length us, event | category | flops | bytes accessed | tf_op | source)
XLA Modules:
  0.0 32.8 jit_solution(10538623939920847630)
XLA Ops:
  0.0 30.9 %shard_map.55 = f32[256,512]{1,0:T(8,128)} custom-call(f32[256,256]{1,0:T(8,128)} %values_hbm.1, f32[256,256]{1,0:T(8,128)} %gates_hbm.1, f32[512,256]{1,0:T(8,128)} %taps_hbm.1, f32[1,256]{1,0:T(1,128)} %bitcast.3, bf16[4,256,512]{2,1,0:T(8,128)(2,1)} %bitcast.2), custom_call_target="tpu_custom_call" | custom-call | tf_op jit(solution)/shard_map/pallas_call | solution.py:382
  30.9 1.9 %copy.7 = f32[256,512]{1,0:T(8,128)} copy(f32[256,512]{1,0:T(8,128)} %shard_map.55) | data formatting | bytes 1048576

commit v4 on v3

--- a/solution.py
+++ b/solution.py
@@ -205,18 +205,20 @@
 
     loads[1].wait()
 
-    def tap_copy(step):
+    def tap_copy(group, step):
         to = lax.rem(me + step, seq_size)
+        part = pl.ds(group * TILE, TILE)
         return pltpu.make_async_remote_copy(
-            h_out.at[to], h_in.at[me], h_send.at[step], h_recv.at[me],
+            h_out.at[to, part], h_in.at[me, part], h_send.at[group, step], h_recv.at[group, me],
             device_id={"seq": to}, device_id_type=MESH,
         )
 
     @pl.when(me < tap_sources)
     def _():
         h_out[...] = taps_ref[...].T.astype(bf16).reshape(h_out.shape)
-        for step in range(1, seq_size):
-            tap_copy(step).start()
+        for group in range(groups):
+            for step in range(1, seq_size):
+                tap_copy(group, step).start()
         h_in[me] = h_out[me]
 
     x_in[me] = x_out[me]
@@ -252,21 +254,24 @@
                 ].astype(f32)
         lax.fori_loop(group * turns, (group + 1) * turns, build, 0)
 
-    for source in range(tap_sources):
-        @pl.when(me != source)
-        def _():
-            pltpu.make_async_remote_copy(
-                h_out.at[0], h_in.at[source], h_send.at[0], h_recv.at[source],
-                device_id={"seq": source}, device_id_type=MESH,
-            ).wait_recv()
-
     pieces = tap_rows // LANES
     flat_blocks = h_blocks.reshape(narrow * 2 * blocks, LANES)
-    for source in range(tap_sources):
-        for piece in range(pieces):
-            flat_blocks[pl.ds(blocks + source * pieces + piece, narrow, stride=2 * blocks), :] = h_in[
-                source, :, piece * LANES : (piece + 1) * LANES
-            ].astype(f32)
+
+    def take_taps(group):
+        part = slice(group * TILE, (group + 1) * TILE)
+        for source in range(tap_sources):
+            @pl.when(me != source)
+            def _():
+                pltpu.make_async_remote_copy(
+                    h_out.at[0, part], h_in.at[source, part], h_send.at[group, 0],
+                    h_recv.at[group, source], device_id={"seq": source}, device_id_type=MESH,
+                ).wait_recv()
+        for source in range(tap_sources):
+            for piece in range(pieces):
+                first = group * TILE * 2 * blocks + blocks + source * pieces + piece
+                flat_blocks[pl.ds(first, TILE, stride=2 * blocks), :] = h_in[
+                    source, part, piece * LANES : (piece + 1) * LANES
+                ].astype(f32)
 
     def convolve_one(channel):
         left = jnp.concatenate(
@@ -281,7 +286,10 @@
             convolve_one(turn * CONV_UNROLL + part)
         return carry
 
-    lax.fori_loop(0, narrow // CONV_UNROLL, convolve, 0)
+    turns = TILE // CONV_UNROLL
+    for group in range(groups):
+        take_taps(group)
+        lax.fori_loop(group * turns, (group + 1) * turns, convolve, 0)
     for block in range(blocks):
         y_out[block // per, :, (block % per) * LANES : (block % per + 1) * LANES] = y_blocks[
             pl.ds(block, narrow, stride=blocks), :
@@ -362,8 +370,9 @@
 
     @pl.when(me < tap_sources)
     def _():
-        for step in range(1, seq_size):
-            tap_copy(step).wait_send()
+        for group in range(groups):
+            for step in range(1, seq_size):
+                tap_copy(group, step).wait_send()
 
 
 def toeplitz_body(values, gates, filter_taps, skip, out_weight):
@@ -405,8 +414,8 @@
             dma((per,)),
             dma((narrow // TILE, seq_size)),
             dma((narrow // TILE, seq_size)),
-            dma((seq_size,)),
-            dma((sources,)),
+            dma((narrow // TILE, seq_size)),
+            dma((narrow // TILE, sources)),
             dma((per, seq_size)),
             dma((per, seq_size)),
             dma((ch_size, per)),

time: 33 us -> 32.4 us (0.982)
  Pallas kernels: 30.9 us -> 30.3 us
    pallas_call x1, Pallas kernels: 30.9 us -> 30.3 us  [toeplitz_body(): pl.pallas_call(functools.partial(toeplitz_kernel, sources), out_shape=jax...]
where the time goes in v4:
time: 32.4 us; the launch traced here: 32.2 us
  Pallas kernels  30.3 us (94%)
  local copies, waits for them, and re-layouts  1.87 us (6%)
    pallas_call x1, Pallas kernels, toeplitz_body(): pl.pallas_call(functools.partial(toeplitz_kernel, sources), out_shape=jax...  30.3 us
    unnamed x1, local copies, waits for them, and re-layouts  1.87 us

profile of v4, /device:TPU:1, one launch (start us, length us, event | category | flops | bytes accessed | tf_op | source)
XLA Modules:
  0.0 32.2 jit_solution(485170445405961947)
XLA Ops:
  0.0 30.3 %shard_map.55 = f32[256,512]{1,0:T(8,128)} custom-call(f32[256,256]{1,0:T(8,128)} %values_hbm.1, f32[256,256]{1,0:T(8,128)} %gates_hbm.1, f32[512,256]{1,0:T(8,128)} %taps_hbm.1, f32[1,256]{1,0:T(1,128)} %bitcast.3, bf16[4,256,512]{2,1,0:T(8,128)(2,1)} %bitcast.2), custom_call_target="tpu_custom_call" | custom-call | tf_op jit(solution)/shard_map/pallas_call | solution.py:391
  30.3 1.9 %copy.7 = f32[256,512]{1,0:T(8,128)} copy(f32[256,512]{1,0:T(8,128)} %shard_map.55) | data formatting | bytes 1048576
